TPU v7x, 32 devices: a whole 2x2x4 slice. The times are simulated.
32 devices in a mesh: dp: 8 (over z, x), mp: 4 (over y, core).
Axes of the slice: x: 2, y: 2, z: 4, core: 2. Of those that a mesh axis runs over, the one named last changes fastest.
Arguments:
- tokens: bfloat16 [8, 196, 1280], P('dp'), may hold values from -6 to 6
- pad_mask: int32 [8, 196], P('dp'), may hold values from 0 to 1, as said below
- cotangent: bfloat16 [8, 196, 1280], P('dp'), may hold values from -6 to 6
- norm_gains: float32 [2, 1280], replicated, may hold values from 0.5 to 1.5
- norm_biases: float32 [2, 1280], replicated, may hold values from -2 to 2
- out_biases: float32 [2, 1280], replicated, may hold values from -2 to 2
- qkv_bias: float32 [3840], P('mp'), may hold values from -2 to 2
- up_bias: float32 [5120], P('mp'), may hold values from -2 to 2
- rel_pos: float32 [2, 27, 80], replicated, may hold values from -0.6 to 0.6
- attn_owner: int32 [4, 64], P('mp'), may hold values from 0 to 63, as said below
- mlp_owner: int32 [4, 128], P('mp'), may hold values from 0 to 127, as said below
- attn_master: float32 [4, 64, 25600], P('mp', 'dp')
- mlp_master: float32 [4, 128, 25600], P('mp', 'dp')
- attn_left: float32 [4, 64, 25600], P('mp', 'dp'), may hold values from -0.5 to 0.5
- attn_right: float32 [4, 64, 25600], P('mp', 'dp'), may hold values from -0.5 to 0.5
- mlp_left: float32 [4, 128, 25600], P('mp', 'dp'), may hold values from -0.5 to 0.5
- mlp_right: float32 [4, 128, 25600], P('mp', 'dp'), may hold values from -0.5 to 0.5
- attn_first: float32 [4, 64, 25600], P('mp', 'dp')
- attn_second: float32 [4, 64, 25600], P('mp', 'dp'), as said below
- mlp_first: float32 [4, 128, 25600], P('mp', 'dp')
- mlp_second: float32 [4, 128, 25600], P('mp', 'dp'), as said below
Outputs:
- block_output: bfloat16 [8, 196, 1280], P('dp')
- tokens_grad: float32 [8, 196, 1280], P('dp')
- gains_grad: float32 [2, 1280], replicated
- biases_grad: float32 [2, 1280], replicated
- out_biases_grad: float32 [2, 1280], replicated
- qkv_bias_grad: float32 [3840], P('mp')
- up_bias_grad: float32 [5120], P('mp')
- rel_pos_grad: float32 [2, 27, 80], replicated
- attn_grad: float32 [4, 64, 25600], P('mp', 'dp')
- mlp_grad: float32 [4, 128, 25600], P('mp', 'dp')
- attn_new: float32 [4, 64, 25600], P('mp', 'dp')
- mlp_new: float32 [4, 128, 25600], P('mp', 'dp')
- attn_copy: bfloat16 [4, 64, 25600], P('mp', 'dp')
- mlp_copy: bfloat16 [4, 128, 25600], P('mp', 'dp')
- attn_first_new: float32 [4, 64, 25600], P('mp', 'dp')
- attn_second_new: float32 [4, 64, 25600], P('mp', 'dp')
- mlp_first_new: float32 [4, 128, 25600], P('mp', 'dp')
- mlp_second_new: float32 [4, 128, 25600], P('mp', 'dp')
Inputs may be any that keep to these rules, and one draw needn't show every extreme that they name: `pad_mask`: slot s holds window s mod (25) of image s // 25, windows row-major in a 5 x 5 grid of 14 x 14 tokens, tokens row-major; slots of images from 1 on are all 0; in each image the 1 entries form a 64 x 64 square at an offset of 0 to 6 rows and columns. `attn_owner`: each row is a permutation of 0 to 63. `mlp_owner`: each row is a permutation of 0 to 127. `attn_second`: every entry is positive. `mlp_second`: every entry is positive.
All inputs are finite; a program needn't handle non-finite values.
Results may differ from a plain program's by a relative error of at most 0.017.
Values may be sent and summed in bfloat16 or wider, within the bound.
A program may use at most 192 MiB of HBM per device.

v0:
```python
import math
import jax
import jax.numpy as jnp
from jax import lax
from jax.sharding import PartitionSpec as P

highest = lax.Precision.HIGHEST
norm_eps = 1e-06
beta_one = 0.9
beta_two = 0.95
adam_eps = 1e-08
learn_rate = 0.02


def untile(tile_rows, row_count, col_count, tile_side):
    shaped = tile_rows.reshape(row_count // tile_side, col_count // tile_side, tile_side, tile_side)
    return shaped.transpose(0, 2, 1, 3).reshape(row_count, col_count)


def retile(matrix, tile_side):
    row_count, col_count = matrix.shape
    shaped = matrix.reshape(row_count // tile_side, tile_side, col_count // tile_side, tile_side)
    return shaped.transpose(0, 2, 1, 3).reshape(-1, tile_side * tile_side)


def rel_onehot(win_side):
    positions = jnp.arange(win_side, dtype=jnp.int32)
    offset = positions[:, None] - positions[None, :] + (win_side - 1)
    entries = jnp.arange(2 * win_side - 1, dtype=jnp.int32)
    return (offset[:, :, None] == entries[None, None, :]).astype(jnp.float32)


def norm_forward(values, norm_gain, norm_shift):
    centre = values - jnp.mean(values, axis=-1, keepdims=True)
    inverse = lax.rsqrt(jnp.mean(centre * centre, axis=-1, keepdims=True) + norm_eps)
    unit_rows = centre * inverse
    return (unit_rows * norm_gain + norm_shift, unit_rows, inverse)


def norm_backward(grad_in, unit_rows, inverse, norm_gain):
    grad_unit = grad_in * norm_gain
    centred = grad_unit - jnp.mean(grad_unit, axis=-1, keepdims=True)
    return inverse * (centred - unit_rows * jnp.mean(grad_unit * unit_rows, axis=-1, keepdims=True))


def gelu_pair(values):
    normal_cdf = 0.5 * (1.0 + lax.erf(values * 0.5**0.5))
    density = jnp.exp(-0.5 * values * values) * (2.0 * math.pi) ** (-0.5)
    return (values * normal_cdf, normal_cdf + values * density)


def soap_step(grad_tiles, master, left_basis, right_basis, first_moment, second_moment):
    tile_side = math.isqrt(grad_tiles.shape[2])
    square = (grad_tiles.shape[0], grad_tiles.shape[1], tile_side, tile_side)
    left_square = left_basis.reshape(square)
    right_square = right_basis.reshape(square)
    half_turn = jnp.einsum(
        "mtji,mtjk->mtik", left_square, grad_tiles.reshape(square), precision=highest
    )
    rotated = jnp.einsum("mtik,mtkl->mtil", half_turn, right_square, precision=highest).reshape(
        grad_tiles.shape
    )
    first_new = beta_one * first_moment + (1.0 - beta_one) * rotated
    second_new = beta_two * second_moment + (1.0 - beta_two) * rotated * rotated
    direction = (first_new / (jnp.sqrt(second_new) + adam_eps)).reshape(square)
    back_half = jnp.einsum("mtij,mtjk->mtik", left_square, direction, precision=highest)
    update = jnp.einsum("mtik,mtlk->mtil", back_half, right_square, precision=highest).reshape(
        grad_tiles.shape
    )
    master_new = master - learn_rate * update
    return (master_new, master_new.astype(jnp.bfloat16), first_new, second_new)


def local(
    tokens,
    pad_mask,
    cotangent,
    norm_gains,
    norm_biases,
    out_biases,
    qkv_bias,
    up_bias,
    rel_pos,
    attn_owner,
    mlp_owner,
    attn_master,
    mlp_master,
    attn_left,
    attn_right,
    mlp_left,
    mlp_right,
    attn_first,
    attn_second,
    mlp_first,
    mlp_second,
):
    windows, win_tokens, model_width = tokens.shape
    row_count = windows * win_tokens
    qkv_cols = qkv_bias.shape[0]
    head_cols = qkv_cols // 3
    unit_cols = up_bias.shape[0]
    head_dim = rel_pos.shape[2]
    heads_here = head_cols // head_dim
    win_side = (rel_pos.shape[1] + 1) // 2
    tile_side = math.isqrt(attn_master.shape[2])
    qkv_count = model_width // tile_side * (qkv_cols // tile_side)
    up_count = model_width // tile_side * (unit_cols // tile_side)
    score_scale = head_dim ** (-0.5)
    attn_stored, mlp_stored = (
        lax.all_gather(attn_master.astype(jnp.bfloat16), "dp", axis=1, tiled=True),
        lax.all_gather(mlp_master.astype(jnp.bfloat16), "dp", axis=1, tiled=True),
    )
    attn_order = jnp.argsort(attn_owner[0])
    mlp_order = jnp.argsort(mlp_owner[0])
    attn_sorted = attn_stored[0][attn_order]
    mlp_sorted = mlp_stored[0][mlp_order]
    w_qkv = untile(attn_sorted[:qkv_count], model_width, qkv_cols, tile_side)
    w_proj = untile(attn_sorted[qkv_count:], head_cols, model_width, tile_side)
    w_up = untile(mlp_sorted[:up_count], model_width, unit_cols, tile_side)
    w_down = untile(mlp_sorted[up_count:], unit_cols, model_width, tile_side)
    onehot = rel_onehot(win_side)
    table_h = jnp.einsum("ijr,rc->ijc", onehot, rel_pos[0], precision=highest)
    table_w = jnp.einsum("ijr,rc->ijc", onehot, rel_pos[1], precision=highest)
    flat_rows = tokens.reshape(row_count, model_width).astype(jnp.float32)
    live_rows = pad_mask.reshape(row_count, 1).astype(jnp.float32)
    normed, unit_one, inverse_one = norm_forward(flat_rows, norm_gains[0], norm_biases[0])
    normed_low = (normed * live_rows).astype(jnp.bfloat16)
    mixed_rows = (jnp.dot(normed_low, w_qkv, preferred_element_type=jnp.float32) + qkv_bias).astype(
        jnp.bfloat16
    )
    head_parts = mixed_rows.reshape(windows, win_tokens, 3, heads_here, head_dim)
    queries = head_parts[:, :, 0]
    key_rows = head_parts[:, :, 1]
    value_rows = head_parts[:, :, 2]
    query_grid = queries.astype(jnp.float32).reshape(
        windows, win_side, win_side, heads_here, head_dim
    )

    def score_rows():
        direct = (
            jnp.einsum("wqhc,wkhc->whqk", queries, key_rows, preferred_element_type=jnp.float32)
            * score_scale
        )
        along_h = jnp.einsum("wabhc,akc->whabk", query_grid, table_h, precision=highest)
        along_w = jnp.einsum("wabhc,blc->whabl", query_grid, table_w, precision=highest)
        return direct + (along_h[..., :, None] + along_w[..., None, :]).reshape(
            windows, heads_here, win_tokens, win_tokens
        )

    scores = score_rows()
    row_top = jnp.max(scores, axis=-1, keepdims=True)
    exponent = jnp.exp(scores - row_top)
    row_total = jnp.sum(exponent, axis=-1, keepdims=True)
    log_total = row_top + jnp.log(row_total)
    probs_low = (exponent / row_total).astype(jnp.bfloat16)
    attended = jnp.einsum(
        "whqk,wkhc->wqhc", probs_low, value_rows, preferred_element_type=jnp.float32
    )
    attended_low = attended.reshape(row_count, head_cols).astype(jnp.bfloat16)
    branch = lax.psum(
        jnp.dot(attended_low, w_proj, preferred_element_type=jnp.float32).astype(jnp.bfloat16), "mp"
    ).astype(jnp.float32)
    middle = flat_rows + branch + out_biases[0]
    second, unit_two, inverse_two = norm_forward(middle, norm_gains[1], norm_biases[1])
    second_low = second.astype(jnp.bfloat16)
    hidden = jnp.dot(second_low, w_up, preferred_element_type=jnp.float32) + up_bias
    active, gelu_slope = gelu_pair(hidden)
    active_low = active.astype(jnp.bfloat16)
    down_sum = lax.psum(
        jnp.dot(active_low, w_down, preferred_element_type=jnp.float32).astype(jnp.bfloat16), "mp"
    ).astype(jnp.float32)
    block_output = (
        ((middle + down_sum + out_biases[1]) * live_rows)
        .astype(jnp.bfloat16)
        .reshape(windows, win_tokens, model_width)
    )
    grad_out = cotangent.reshape(row_count, model_width).astype(jnp.float32) * live_rows
    grad_out_low = grad_out.astype(jnp.bfloat16)
    down_bias_grad = jnp.sum(grad_out, axis=0)
    w_down_grad = jnp.einsum(
        "nf,nd->fd", active_low, grad_out_low, preferred_element_type=jnp.float32
    )
    grad_active = jnp.einsum("nd,fd->nf", grad_out_low, w_down, preferred_element_type=jnp.float32)
    grad_hidden = (grad_active * gelu_slope).astype(jnp.bfloat16)
    up_bias_grad = jnp.sum(grad_hidden.astype(jnp.float32), axis=0)
    w_up_grad = jnp.einsum("nd,nf->df", second_low, grad_hidden, preferred_element_type=jnp.float32)
    mlp_stack = jnp.concatenate(
        [retile(w_up_grad, tile_side), retile(w_down_grad, tile_side)], axis=0
    )[mlp_owner[0]][None]
    grad_second = lax.psum(
        jnp.einsum("nf,df->nd", grad_hidden, w_up, preferred_element_type=jnp.float32).astype(
            jnp.bfloat16
        ),
        "mp",
    ).astype(jnp.float32)
    gain_two_grad = jnp.sum(grad_second * unit_two, axis=0)
    shift_two_grad = jnp.sum(grad_second, axis=0)
    grad_middle = grad_out + norm_backward(grad_second, unit_two, inverse_two, norm_gains[1])
    proj_bias_grad = jnp.sum(grad_middle, axis=0)
    grad_branch = grad_middle.astype(jnp.bfloat16)
    w_proj_grad = jnp.einsum(
        "nc,nd->cd", attended_low, grad_branch, preferred_element_type=jnp.float32
    )
    grad_attended = jnp.einsum("nd,cd->nc", grad_branch, w_proj, preferred_element_type=jnp.float32)
    grad_attended = grad_attended.astype(jnp.bfloat16).reshape(
        windows, win_tokens, heads_here, head_dim
    )
    probs_full = jnp.exp(score_rows() - log_total)
    probs_again = probs_full.astype(jnp.bfloat16)
    grad_probs = jnp.einsum(
        "wqhc,wkhc->whqk", grad_attended, value_rows, preferred_element_type=jnp.float32
    )
    grad_values = jnp.einsum(
        "whqk,wqhc->wkhc", probs_again, grad_attended, preferred_element_type=jnp.float32
    )
    grad_scores = (
        probs_full * (grad_probs - jnp.sum(probs_full * grad_probs, axis=-1, keepdims=True))
    ).astype(jnp.bfloat16)
    grad_queries = (
        jnp.einsum("whqk,wkhc->wqhc", grad_scores, key_rows, preferred_element_type=jnp.float32)
        * score_scale
    )
    grad_keys = (
        jnp.einsum("whqk,wqhc->wkhc", grad_scores, queries, preferred_element_type=jnp.float32)
        * score_scale
    )
    grad_grid = grad_scores.astype(jnp.float32).reshape(
        windows, heads_here, win_side, win_side, win_side, win_side
    )
    grad_h = jnp.sum(grad_grid, axis=5)
    grad_w = jnp.sum(grad_grid, axis=4)
    grad_rel_q = jnp.einsum("whabk,akc->wabhc", grad_h, table_h, precision=highest) + jnp.einsum(
        "whabl,blc->wabhc", grad_w, table_w, precision=highest
    )
    grad_queries = grad_queries + grad_rel_q.reshape(windows, win_tokens, heads_here, head_dim)
    table_h_grad = jnp.einsum("whabk,wabhc->akc", grad_h, query_grid, precision=highest)
    table_w_grad = jnp.einsum("whabl,wabhc->blc", grad_w, query_grid, precision=highest)
    rel_part = jnp.stack(
        [
            jnp.einsum("ijr,ijc->rc", onehot, table_h_grad, precision=highest),
            jnp.einsum("ijr,ijc->rc", onehot, table_w_grad, precision=highest),
        ]
    )
    grad_mixed = (
        jnp.stack([grad_queries, grad_keys, grad_values], axis=2)
        .reshape(row_count, qkv_cols)
        .astype(jnp.bfloat16)
    )
    qkv_bias_grad = jnp.sum(grad_mixed.astype(jnp.float32), axis=0)
    w_qkv_grad = jnp.einsum("nd,nc->dc", normed_low, grad_mixed, preferred_element_type=jnp.float32)
    grad_normed, rel_sum = (
        lax.psum(
            jnp.einsum("nc,dc->nd", grad_mixed, w_qkv, preferred_element_type=jnp.float32).astype(
                jnp.bfloat16
            ),
            "mp",
        ).astype(jnp.float32),
        lax.psum(rel_part.astype(jnp.bfloat16), "mp").astype(jnp.float32),
    )
    grad_normed = grad_normed * live_rows
    gain_one_grad = jnp.sum(grad_normed * unit_one, axis=0)
    shift_one_grad = jnp.sum(grad_normed, axis=0)
    tokens_grad = (
        grad_middle + norm_backward(grad_normed, unit_one, inverse_one, norm_gains[0])
    ).reshape(windows, win_tokens, model_width)
    attn_stack = jnp.concatenate(
        [retile(w_qkv_grad, tile_side), retile(w_proj_grad, tile_side)], axis=0
    )[attn_owner[0]][None]
    attn_grad, mlp_grad = (
        lax.psum_scatter(attn_stack, "dp", scatter_dimension=1, tiled=True),
        lax.psum_scatter(mlp_stack, "dp", scatter_dimension=1, tiled=True),
    )
    gains_grad, biases_grad, out_biases_grad, rel_pos_grad, qkv_bias_total, up_bias_total = (
        lax.psum(
            (
                jnp.stack([gain_one_grad, gain_two_grad]),
                jnp.stack([shift_one_grad, shift_two_grad]),
                jnp.stack([proj_bias_grad, down_bias_grad]),
                rel_sum,
                qkv_bias_grad,
                up_bias_grad,
            ),
            "dp",
        )
    )
    attn_new, attn_copy, attn_first_new, attn_second_new = soap_step(
        attn_grad, attn_master, attn_left, attn_right, attn_first, attn_second
    )
    mlp_new, mlp_copy, mlp_first_new, mlp_second_new = soap_step(
        mlp_grad, mlp_master, mlp_left, mlp_right, mlp_first, mlp_second
    )
    return (
        block_output,
        tokens_grad,
        gains_grad,
        biases_grad,
        out_biases_grad,
        qkv_bias_total,
        up_bias_total,
        rel_pos_grad,
        attn_grad,
        mlp_grad,
        attn_new,
        mlp_new,
        attn_copy,
        mlp_copy,
        attn_first_new,
        attn_second_new,
        mlp_first_new,
        mlp_second_new,
    )


def solution(mesh):
    placed = (
        P("dp", None, None),
        P("dp", None),
        P("dp", None, None),
        P(),
        P(),
        P(),
        P("mp"),
        P("mp"),
        P(),
        P("mp", None),
        P("mp", None),
        P("mp", "dp", None),
        P("mp", "dp", None),
        P("mp", "dp", None),
        P("mp", "dp", None),
        P("mp", "dp", None),
        P("mp", "dp", None),
        P("mp", "dp", None),
        P("mp", "dp", None),
        P("mp", "dp", None),
        P("mp", "dp", None),
    )
    return jax.shard_map(
        local,
        mesh=mesh,
        in_specs=placed,
        out_specs=(
            P("dp", None, None),
            P("dp", None, None),
            P(),
            P(),
            P(),
            P("mp"),
            P("mp"),
            P(),
            P("mp", "dp", None),
            P("mp", "dp", None),
            P("mp", "dp", None),
            P("mp", "dp", None),
            P("mp", "dp", None),
            P("mp", "dp", None),
            P("mp", "dp", None),
            P("mp", "dp", None),
            P("mp", "dp", None),
            P("mp", "dp", None),
        ),
        check_vma=False,
    )
```

profile of v0, /device:TPU:0, one launch (start us, length us, event | category | flops | bytes accessed | tf_op | source)
XLA Modules:
  0.0 886.3 jit_solution(16054658435756151305)
XLA Ops:
  17.7 57.3 %all-gather.3.cloned.1.call-done = bf16[1,64,25600]{2,1,0:T(8,128)(2,1)} async-done(((bf16[1,8,25600]{2,1,0:T(8,128)(2,1)}), bf16[1,64,25600]{2,1,0:T(8,128)(2,1)}) %all-gather.3.cloned.1.call-update) | async-done | bytes 3276816 | tf_op jit(solution)/shard_map/all_gather | solution.py:110
  75.0 9.5 %gather_fusion = bf16[64,25600]{1,0:T(8,128)(2,1)} fusion(bf16[64,25600]{1,0:T(8,128)(2,1)} %bitcast.343, s32[1024]{0:T(1024)S(1)} %pad_clamp_fusion.3), kind=kCustom, calls=%fused_computation | custom fusion | bytes 6553856 | tf_op jit(solution)/shard_map/gather | solution.py:115
  140.4 26.9 %all-reduce.6.cloned.1.call-done = bf16[196,1280]{1,0:T(8,128)(2,1)} async-done(((bf16[196,1280]{1,0:T(8,128)(2,1)}), bf16[196,1280]{1,0:T(8,128)(2,1)}) %all-reduce.6.cloned.1.call-update) | async-done | bytes 501776 | tf_op jit(solution)/shard_map/psum | solution.py:160
  170.0 102.3 %all-gather.5.cloned.1.call-done = bf16[1,128,25600]{2,1,0:T(8,128)(2,1)} async-done(((bf16[1,16,25600]{2,1,0:T(8,128)(2,1)}), bf16[1,128,25600]{2,1,0:T(8,128)(2,1)}) %all-gather.5.cloned.1.call-update) | async-done | bytes 6553616 | tf_op jit(solution)/shard_map/all_gather | solution.py:111
  272.2 17.0 %gather_fusion.1 = bf16[128,25600]{1,0:T(8,128)(2,1)} fusion(bf16[128,25600]{1,0:T(8,128)(2,1)} %bitcast.342, s32[1024]{0:T(1024)S(1)} %pad_clamp_fusion.2), kind=kCustom, calls=%fused_computation.1 | custom fusion | bytes 13107712 | tf_op jit(solution)/shard_map/gather | solution.py:116
  295.3 9.7 %reshape.655 = bf16[8,8,160,160]{3,2,1,0:T(8,128)(2,1)} reshape(bf16[64,25600]{1,0:T(8,128)(2,1)} %get-tuple-element.115) | data formatting | bytes 6553600 | tf_op jit(solution)/shard_map/reshape | solution.py:16
  305.0 8.0 copy.177
  313.0 9.2 %reshape.656 = bf16[1280,1280]{1,0:T(8,128)(2,1)} reshape(bf16[8,160,8,160]{3,2,1,0:T(8,128)(2,1)} %bitcast.347) | data formatting | bytes 6553600 | tf_op jit(solution)/shard_map/reshape | solution.py:17
  322.2 9.7 %reshape.657 = bf16[8,8,160,160]{3,2,1,0:T(8,128)(2,1)} reshape(bf16[64,25600]{1,0:T(8,128)(2,1)} %get-tuple-element.116) | data formatting | bytes 6553600 | tf_op jit(solution)/shard_map/reshape | solution.py:16
  339.8 9.6 %reshape.658 = bf16[1280,1280]{1,0:T(8,128)(2,1)} reshape(bf16[8,160,8,160]{3,2,1,0:T(8,128)(2,1)} %bitcast.348) | data formatting | bytes 6553600 | tf_op jit(solution)/shard_map/reshape | solution.py:17
  362.2 27.6 %all-reduce.8.cloned.1.call-done = bf16[196,1280]{1,0:T(8,128)(2,1)} async-done(((bf16[196,1280]{1,0:T(8,128)(2,1)}), bf16[196,1280]{1,0:T(8,128)(2,1)}) %all-reduce.8.cloned.1.call-update) | async-done | bytes 501776 | tf_op jit(solution)/shard_map/psum | solution.py:190
  430.9 27.0 %all-reduce.10.cloned.1.call-done = (bf16[196,1280]{1,0:T(8,128)(2,1)}, bf16[196,1280]{1,0:T(8,128)(2,1)}) async-done(((bf16[196,1280]{1,0:T(8,128)(2,1)}, bf16[196,1280]{1,0:T(8,128)(2,1)}), (bf16[196,1280]{1,0:T(8,128)(2,1)}, bf16[196,1280]{1,0:T(8,128)(2,1)})) %all-reduce.10.cloned.1.call-update) | async-done | bytes 1003536 | tf_op jit(solution)/shard_map/psum | solution.py:169
  468.3 9.4 %reshape.665 = f32[48,25600]{1,0:T(8,128)} reshape(f32[8,6,160,160]{3,2,1,0:T(8,128)} %convolution_bitcast_fusion.1) | data formatting | bytes 9830400 | tf_op jit(solution)/shard_map/reshape | solution.py:23
  483.3 10.7 %gather_fusion.2 = f32[64,25600]{1,0:T(8,128)} fusion(f32[64,25600]{1,0:T(8,128)} %pad_maximum_fusion.1, s32[1024]{0:T(1024)S(1)} %pad_clamp_fusion.1), kind=kCustom, calls=%fused_computation.2 | custom fusion | bytes 13107456 | tf_op jit(solution)/shard_map/gather | solution.py:266
  499.5 11.1 %reshape.667 = f32[8,160,8,160]{3,2,1,0:T(8,128)} reshape(f32[1280,1280]{1,0:T(8,128)} %fusion.96) | data formatting | bytes 13107200 | tf_op jit(solution)/shard_map/reshape | solution.py:22
  510.6 11.2 %copy.122 = f32[8,8,160,160]{3,2,1,0:T(8,128)} copy(f32[8,8,160,160]{3,1,2,0:T(8,128)} %bitcast.345) | data formatting | bytes 13107200 | tf_op jit(solution)/shard_map/transpose | solution.py:23
  521.7 12.1 %reshape.668 = f32[64,25600]{1,0:T(8,128)} reshape(f32[8,8,160,160]{3,2,1,0:T(8,128)} %copy.122) | data formatting | bytes 13107200 | tf_op jit(solution)/shard_map/reshape | solution.py:23
  539.5 12.0 %reshape.669 = f32[64,25600]{1,0:T(8,128)} reshape(f32[8,8,160,160]{3,2,1,0:T(8,128)} %convolution_bitcast_fusion) | data formatting | bytes 13107200 | tf_op jit(solution)/shard_map/reshape | solution.py:23
  551.6 11.0 %pad_maximum_fusion = f32[128,25600]{1,0:T(8,128)} fusion(f32[64,25600]{1,0:T(8,128)} %reshape.669, f32[64,25600]{1,0:T(8,128)} %reshape.668), kind=kLoop, calls=%fused_computation.4 | loop fusion | flops 3276800 | bytes 26214400 | tf_op jit(solution)/shard_map/concatenate | solution.py:187
  562.6 19.3 %gather_fusion.3 = f32[128,25600]{1,0:T(8,128)} fusion(f32[128,25600]{1,0:T(8,128)} %pad_maximum_fusion, s32[1024]{0:T(1024)S(1)} %pad_clamp_fusion), kind=kCustom, calls=%fused_computation.3 | custom fusion | bytes 26214912 | tf_op jit(solution)/shard_map/gather | solution.py:187
  595.0 11.3 %psum.86 = bf16[2,27,80]{2,1,0:T(8,128)(2,1)S(1)} all-reduce(bf16[2,27,80]{2,1,0:T(8,128)(2,1)S(1)} %pad_maximum_fusion.2), channel_id=1, replica_groups=mesh['dp'=8,'mp'=4] {'mp'}, use_global_device_ids=true, to_apply=%region_32.33 | all-reduce | flops 4320 | bytes 17280 | tf_op jit(solution)/shard_map/psum | solution.py:258
  609.6 40.8 %all-reduce = (f32[2,1280]{1,0:T(2,128)}, f32[2,1280]{1,0:T(2,128)}, f32[2,1280]{1,0:T(2,128)}, f32[960]{0:T(1024)}, f32[1280]{0:T(1024)}, /*index=5*/f32[2,27,80]{2,1,0:T(8,128)S(1)}) all-reduce(f32[2,1280]{1,0:T(2,128)S(1)} %pad_maximum_fusion.3, f32[2,1280]{1,0:T(2,128)S(1)} %pad_maximum_fusion.4, ...), channel_id=1, replica_groups=mesh['dp'=8,'mp'=4] {'dp'}, use_global_device_ids=true, to_apply=%region_21.22 | all-reduce | flops 14240 | bytes 105280 | tf_op jit(solution)/shard_map/psum | solution.py:274
  680.3 154.9 %reduce-scatter.5.cloned.1.call-done = f32[1,16,25600]{2,1,0:T(8,128)} async-done(((f32[1,128,25600]{2,1,0:T(8,128)}), f32[1,16,25600]{2,1,0:T(8,128)}) %reduce-scatter.5.cloned.1.call-update) | async-done | bytes 1638416 | tf_op jit(solution)/shard_map/reduce_scatter | solution.py:271
  839.1 8.1 fusion.111
  (247 shorter events, 245.3 us)
Async XLA Ops:
  7.2 10.2 %copy-start = (bf16[1,196,1280]{2,1,0:T(8,128)(2,1)S(1)}, bf16[1,196,1280]{2,1,0:T(8,128)(2,1)}, u32[]{:S(2)}) copy-start(bf16[1,196,1280]{2,1,0:T(8,128)(2,1)} %param.21) | copy-start | bytes 1505284
  7.2 67.8 %all-gather.3.cloned.1.call-start = ((), (), s32[]{:S(2)}) async-start(), calls=%async_computation.2 | async-start | bytes 3686400 | tf_op jit(solution)/shard_map/all_gather | solution.py:110
  9.3 158.1 %all-reduce.6.cloned.1.call-start = ((), (), s32[]{:S(2)}) async-start(), calls=%async_computation.3 | async-start | bytes 1024000 | tf_op jit(solution)/shard_map/psum | solution.py:160
  10.0 381.5 %copy-start.37 = (f32[1,196]{1,0:T(1,128)}, f32[1,196]{1,0:T(1,128)S(1)}, u32[]{:S(2)}) copy-start(f32[1,196]{1,0:T(1,128)S(1)} %convert_element_type.176) | copy-start | bytes 2356
  17.4 88.4 %copy-start.35 = (f32[196]{0:T(256)}, f32[196]{0:T(256)S(1)}, u32[]{:S(2)}) copy-start(f32[196]{0:T(256)S(1)} %broadcast_multiply_fusion.5) | copy-start | bytes 2356
  17.7 88.1 %copy-start.40 = (f32[196]{0:T(256)}, f32[196]{0:T(256)S(1)}, u32[]{:S(2)}) copy-start(f32[196]{0:T(256)S(1)} %add_rsqrt_fusion.1) | copy-start | bytes 2356
  108.8 288.4 %copy-start.15 = (bf16[196,960]{0,1:T(8,128)(2,1)}, bf16[196,960]{0,1:T(8,128)(2,1)S(1)}, u32[]{:S(2)}) copy-start(bf16[196,960]{0,1:T(8,128)(2,1)S(1)} %copy.93) | copy-start | bytes 1128964
  109.0 10.2 %copy-start.11 = (bf16[1,196,1,4,80]{4,3,1,2,0:T(4,128)(2,1)}, bf16[1,196,1,4,80]{4,3,1,2,0:T(4,128)(2,1)S(1)}, u32[]{:S(2)}) copy-start(bf16[1,196,1,4,80]{4,3,1,2,0:T(4,128)(2,1)S(1)} %copy.95) | copy-start | bytes 376324
  135.1 137.2 %all-gather.5.cloned.1.call-start = ((), (), s32[]{:S(2)}) async-start(), calls=%async_computation.4 | async-start | bytes 7372800 | tf_op jit(solution)/shard_map/all_gather | solution.py:111
  137.6 252.3 %all-reduce.8.cloned.1.call-start = ((), (), s32[]{:S(2)}) async-start(), calls=%async_computation.5 | async-start | bytes 1024000 | tf_op jit(solution)/shard_map/psum | solution.py:190
  339.8 9.6 %copy-start.1 = (bf16[196,1280]{1,0:T(8,128)(2,1)S(1)}, bf16[196,1280]{1,0:T(8,128)(2,1)}, u32[]{:S(2)}) copy-start(bf16[196,1280]{1,0:T(8,128)(2,1)} %all-reduce.6.cloned.1.call-done) | copy-start | bytes 1505284
  339.8 9.6 %copy-start.43 = (f32[1280]{0:T(1024)S(1)}, f32[1280]{0:T(1024)}, u32[]{:S(2)}) copy-start(f32[1280]{0:T(1024)} %param.28) | copy-start | bytes 15364
  358.2 99.7 %all-reduce.10.cloned.1.call-start = ((), (), s32[]{:S(2)}) async-start(), calls=%async_computation.8 | async-start | bytes 2048000 | tf_op jit(solution)/shard_map/psum | solution.py:169
  411.0 8.8 copy-start.5
  421.4 229.6 %reduce-scatter.3.cloned.1.call-start = ((), (), s32[]{:S(2)}) async-start(), calls=%async_computation.6 | async-start | bytes 7372800 | tf_op jit(solution)/shard_map/reduce_scatter | solution.py:270
  426.3 31.6 %copy-start.23 = (bf16[1,196,1280]{2,1,0:T(8,128)(2,1)S(1)}, bf16[1,196,1280]{2,1,0:T(8,128)(2,1)}, u32[]{:S(2)}) copy-start(bf16[1,196,1280]{2,1,0:T(8,128)(2,1)} %param.23) | copy-start | bytes 1505284
  426.3 31.6 %copy-start.36 = (f32[196]{0:T(256)S(1)}, f32[196]{0:T(256)}, u32[]{:S(2)}) copy-start(f32[196]{0:T(256)} %copy-done.35) | copy-start | bytes 2356
  426.3 31.6 %copy-start.38 = (f32[1,196]{1,0:T(1,128)S(1)}, f32[1,196]{1,0:T(1,128)}, u32[]{:S(2)}) copy-start(f32[1,196]{1,0:T(1,128)} %copy-done.37) | copy-start | bytes 2356
  426.3 31.6 %copy-start.41 = (f32[196]{0:T(256)S(1)}, f32[196]{0:T(256)}, u32[]{:S(2)}) copy-start(f32[196]{0:T(256)} %copy-done.40) | copy-start | bytes 2356
  426.3 34.0 %copy-start.7 = (f32[196,1280]{1,0:T(8,128)S(1)}, f32[196,1280]{1,0:T(8,128)}, u32[]{:S(2)}) copy-start(f32[196,1280]{1,0:T(8,128)} %copy-done.6) | copy-start | bytes 3010564
  468.3 9.4 %copy-start.8 = (f32[16,25600]{1,0:T(8,128)S(1)}, f32[16,25600]{1,0:T(8,128)}, u32[]{:S(2)}) copy-start(f32[16,25600]{1,0:T(8,128)} %reshape.666) | copy-start | bytes 4915204
  494.1 341.1 %reduce-scatter.5.cloned.1.call-start = ((), (), s32[]{:S(2)}) async-start(), calls=%async_computation.7 | async-start | bytes 14745600 | tf_op jit(solution)/shard_map/reduce_scatter | solution.py:271
  521.7 12.2 %copy-start.21 = (bf16[1280,196]{0,1:T(8,128)(2,1)S(1)}, bf16[1280,196]{0,1:T(8,128)(2,1)}, u32[]{:S(2)}) copy-start(bf16[1280,196]{0,1:T(8,128)(2,1)} %get-tuple-element.121) | copy-start | bytes 1505284
  591.9 17.6 %copy-start.42 = (f32[1280]{0:T(1024)S(1)}, f32[1280]{0:T(1024)}, u32[]{:S(2)}) copy-start(f32[1280]{0:T(1024)} %get-tuple-element.128) | copy-start | bytes 15364
  (33 other events, 108.7 us)
Sparse Core Ops, SparseCore 0:
  10.8 64.1 all-gather.2
  135.2 32.0 all-reduce.5
  170.1 102.1 all-gather.4
  358.3 31.4 all-reduce.7
  421.5 36.3 all-reduce.9
  494.2 122.6 reduce-scatter.2
  621.1 214.0 reduce-scatter.4
where the time goes:
time: 895 us; the launch traced here: 886 us
  waiting for transfers between devices  396 us (44%)
  local copies, waits for them, and re-layouts  271 us (30%)
  matrix products  85.6 us (10%)
  other arithmetic  65.3 us (7%)
  blocking collectives  52.1 us (6%)
  between operations  15.3 us (2%)
    reduce_scatter x1, waiting for transfers between devices, local(): lax.psum_scatter(mlp_stack, 'dp', scatter_dimension=1, tiled=True)  155 us
    all_gather x1, waiting for transfers between devices, local(): lax.all_gather(mlp_master.astype(jnp.bfloat16), 'dp', axis=1, tiled=True)  102 us
    all_gather x1, waiting for transfers between devices, local(): lax.all_gather(attn_master.astype(jnp.bfloat16), 'dp', axis=1, tiled=True)  57.3 us
    reshape x8, local copies, waits for them, and re-layouts, untile(): tile_rows.reshape(row_count // tile_side, col_count // tile_side, tile_si...  54.3 us
    psum x1, blocking collectives, local(): lax.psum((jnp.stack([gain_one_grad, gain_two_grad]), jnp.stack([shift_one...  40.8 us
    reshape x4, local copies, waits for them, and re-layouts, retile(): return shaped.transpose(0, 2, 1, 3).reshape(-1, tile_side * tile_side)  38.1 us
    psum x1, waiting for transfers between devices, local(): lax.psum(jnp.einsum('nf,df->nd', grad_hidden, w_up, preferred_element_typ...  27.6 us
    reshape x4, local copies, waits for them, and re-layouts, untile(): return shaped.transpose(0, 2, 1, 3).reshape(row_count, col_count)  27.4 us
  transfers between devices with their start and end apart: 7, of which 6 were waited for; matrix products, arithmetic and copies ran while one was open for 18% of the time, Pallas kernels for 0%

commit v1 on v0

--- a/solution.py
+++ b/solution.py
@@ -94,6 +94,35 @@
     mlp_first,
     mlp_second,
 ):
+
+    def direct_the_spots(content, bus_axis):
+        value_now, q_next, local_part = (
+            lax.axis_size(bus_axis),
+            lax.axis_index(bus_axis),
+            content.shape[1],
+        )
+        in_order = list(map(lambda idx: (idx, (idx + 1) % value_now), range(value_now)))
+        pieces_in = list(map(lambda idx: (idx, (idx - 1) % value_now), range(value_now)))
+        z = jnp.zeros(
+            (*content.shape[:1], value_now * local_part, *content.shape[2:]), content.dtype
+        )
+        z = lax.dynamic_update_slice_in_dim(z, content, q_next * local_part, axis=1)
+        parts_out = field_out = content
+        big = value_now // 2
+        dev = 1
+        while dev < big + 1:
+            parts_out = lax.ppermute(parts_out, bus_axis, in_order)
+            z = lax.dynamic_update_slice_in_dim(
+                z, parts_out, (q_next - dev) % value_now * local_part, axis=1
+            )
+            if dev < value_now - big:
+                field_out = lax.ppermute(field_out, bus_axis, pieces_in)
+                z = lax.dynamic_update_slice_in_dim(
+                    z, field_out, (q_next + dev) % value_now * local_part, axis=1
+                )
+            dev += 1
+        return z
+
     windows, win_tokens, model_width = tokens.shape
     row_count = windows * win_tokens
     qkv_cols = qkv_bias.shape[0]
@@ -107,7 +136,7 @@
     up_count = model_width // tile_side * (unit_cols // tile_side)
     score_scale = head_dim ** (-0.5)
     attn_stored, mlp_stored = (
-        lax.all_gather(attn_master.astype(jnp.bfloat16), "dp", axis=1, tiled=True),
+        direct_the_spots(attn_master.astype(jnp.bfloat16), bus_axis="dp"),
         lax.all_gather(mlp_master.astype(jnp.bfloat16), "dp", axis=1, tiled=True),
     )
     attn_order = jnp.argsort(attn_owner[0])

time: 895 us -> 861 us (0.962)
  waiting for transfers between devices: 396 us -> 348 us
  starting transfers between devices: 0.46 us -> 19.9 us
    all_gather x1 -> x0, waiting for transfers between devices: 57.3 us -> none  [local(): lax.all_gather(attn_master.astype(jnp.bfloat16), 'dp', axis=1, tiled=True)]
    ppermute x0 -> x7, waiting for transfers between devices: none -> 42.8 us  [the longest x4 42.8 us: direct_the_spots(): parts_out = lax.ppermute(parts_out, bus_axis, in_order)]
    all_gather x1, waiting for transfers between devices: 102 us -> 68.8 us  [local(): lax.all_gather(mlp_master.astype(jnp.bfloat16), 'dp', axis=1, tiled=True)]
    ppermute x0 -> x7, starting transfers between devices: none -> 19.4 us  [the longest x4 10.3 us: direct_the_spots(): parts_out = lax.ppermute(parts_out, bus_axis, in_order)]
  transfers between devices with their start and end apart: 7 -> 13, of which waited for: 6 -> 9; matrix products, arithmetic and copies ran while one was open for 18% -> 19% of each run, Pallas kernels for 0% -> 0%
where the time goes in v1:
time: 861 us; the launch traced here: 854 us
  waiting for transfers between devices  348 us (40%)
  local copies, waits for them, and re-layouts  268 us (31%)
  matrix products  85.6 us (10%)
  other arithmetic  63.9 us (7%)
  blocking collectives  52 us (6%)
  starting transfers between devices  19.9 us (2%)
  between operations  16.9 us (2%)
    reduce_scatter x1, waiting for transfers between devices, local(): lax.psum_scatter(mlp_stack, 'dp', scatter_dimension=1, tiled=True)  155 us
    all_gather x1, waiting for transfers between devices, local(): lax.all_gather(mlp_master.astype(jnp.bfloat16), 'dp', axis=1, tiled=True)  68.8 us
    reshape x8, local copies, waits for them, and re-layouts, untile(): tile_rows.reshape(row_count // tile_side, col_count // tile_side, tile_si...  54.3 us
    ppermute x4, waiting for transfers between devices, direct_the_spots(): parts_out = lax.ppermute(parts_out, bus_axis, in_order)  42.8 us
    psum x1, blocking collectives, local(): lax.psum((jnp.stack([gain_one_grad, gain_two_grad]), jnp.stack([shift_one...  40.7 us
    reshape x4, local copies, waits for them, and re-layouts, retile(): return shaped.transpose(0, 2, 1, 3).reshape(-1, tile_side * tile_side)  38.1 us
    psum x1, waiting for transfers between devices, local(): lax.psum(jnp.einsum('nf,df->nd', grad_hidden, w_up, preferred_element_typ...  27.6 us
    reshape x4, local copies, waits for them, and re-layouts, untile(): return shaped.transpose(0, 2, 1, 3).reshape(row_count, col_count)  27.5 us
  transfers between devices with their start and end apart: 13, of which 9 were waited for; matrix products, arithmetic and copies ran while one was open for 19% of the time, Pallas kernels for 0%

profile of v1, /device:TPU:0, one launch (start us, length us, event | category | flops | bytes accessed | tf_op | source)
XLA Modules:
  0.0 854.0 jit_solution(16467154687473142844)
XLA Ops:
  38.4 11.8 %collective-permute-done.2 = bf16[1,8,25600]{2,1,0:T(8,128)(2,1)S(1)} collective-permute-done((bf16[1,8,25600]{2,1,0:T(8,128)(2,1)}, bf16[1,8,25600]{2,1,0:T(8,128)(2,1)S(1)}, u32[]{:S(2)}, u32[]{:S(2)}) %collective-permute-start.2) | collective-permute-done | bytes 409632 | tf_op jit(solution)/shard_map/ppermute | solution.py:114
  55.8 12.8 %collective-permute-done.4 = bf16[1,8,25600]{2,1,0:T(8,128)(2,1)S(1)} collective-permute-done((bf16[1,8,25600]{2,1,0:T(8,128)(2,1)S(1)}, bf16[1,8,25600]{2,1,0:T(8,128)(2,1)S(1)}, u32[]{:S(2)}, u32[]{:S(2)}) %collective-permute-start.4) | collective-permute-done | bytes 409632 | tf_op jit(solution)/shard_map/ppermute | solution.py:114
  71.2 10.0 %collective-permute-done.6 = bf16[1,8,25600]{2,1,0:T(8,128)(2,1)S(1)} collective-permute-done((bf16[1,8,25600]{2,1,0:T(8,128)(2,1)S(1)}, bf16[1,8,25600]{2,1,0:T(8,128)(2,1)S(1)}, u32[]{:S(2)}, u32[]{:S(2)}) %collective-permute-start.6) | collective-permute-done | bytes 409632 | tf_op jit(solution)/shard_map/ppermute | solution.py:114
  141.7 26.7 %all-reduce.6.cloned.1.call-done = bf16[196,1280]{1,0:T(8,128)(2,1)} async-done(((bf16[196,1280]{1,0:T(8,128)(2,1)}), bf16[196,1280]{1,0:T(8,128)(2,1)}) %all-reduce.6.cloned.1.call-update) | async-done | bytes 501776 | tf_op jit(solution)/shard_map/psum | solution.py:189
  171.0 68.8 %all-gather.2.cloned.1.call-done = bf16[1,128,25600]{2,1,0:T(8,128)(2,1)} async-done(((bf16[1,16,25600]{2,1,0:T(8,128)(2,1)}), bf16[1,128,25600]{2,1,0:T(8,128)(2,1)}) %all-gather.2.cloned.1.call-update) | async-done | bytes 6553616 | tf_op jit(solution)/shard_map/all_gather | solution.py:140
  239.8 17.0 %gather_fusion.1 = bf16[128,25600]{1,0:T(8,128)(2,1)} fusion(bf16[128,25600]{1,0:T(8,128)(2,1)} %bitcast.357, s32[1024]{0:T(1024)S(1)} %pad_clamp_fusion.2), kind=kCustom, calls=%fused_computation.1 | custom fusion | bytes 13107712 | tf_op jit(solution)/shard_map/gather | solution.py:145
  262.9 9.7 %reshape.671 = bf16[8,8,160,160]{3,2,1,0:T(8,128)(2,1)} reshape(bf16[64,25600]{1,0:T(8,128)(2,1)} %get-tuple-element.117) | data formatting | bytes 6553600 | tf_op jit(solution)/shard_map/reshape | solution.py:16
  280.6 9.2 %reshape.672 = bf16[1280,1280]{1,0:T(8,128)(2,1)} reshape(bf16[8,160,8,160]{3,2,1,0:T(8,128)(2,1)} %bitcast.361) | data formatting | bytes 6553600 | tf_op jit(solution)/shard_map/reshape | solution.py:17
  289.8 9.7 %reshape.673 = bf16[8,8,160,160]{3,2,1,0:T(8,128)(2,1)} reshape(bf16[64,25600]{1,0:T(8,128)(2,1)} %get-tuple-element.118) | data formatting | bytes 6553600 | tf_op jit(solution)/shard_map/reshape | solution.py:16
  307.4 9.6 %reshape.674 = bf16[1280,1280]{1,0:T(8,128)(2,1)} reshape(bf16[8,160,8,160]{3,2,1,0:T(8,128)(2,1)} %bitcast.362) | data formatting | bytes 6553600 | tf_op jit(solution)/shard_map/reshape | solution.py:17
  329.8 27.6 %all-reduce.8.cloned.1.call-done = bf16[196,1280]{1,0:T(8,128)(2,1)} async-done(((bf16[196,1280]{1,0:T(8,128)(2,1)}), bf16[196,1280]{1,0:T(8,128)(2,1)}) %all-reduce.8.cloned.1.call-update) | async-done | bytes 501776 | tf_op jit(solution)/shard_map/psum | solution.py:219
  398.4 27.0 %all-reduce.10.cloned.1.call-done = (bf16[196,1280]{1,0:T(8,128)(2,1)}, bf16[196,1280]{1,0:T(8,128)(2,1)}) async-done(((bf16[196,1280]{1,0:T(8,128)(2,1)}, bf16[196,1280]{1,0:T(8,128)(2,1)}), (bf16[196,1280]{1,0:T(8,128)(2,1)}, bf16[196,1280]{1,0:T(8,128)(2,1)})) %all-reduce.10.cloned.1.call-update) | async-done | bytes 1003536 | tf_op jit(solution)/shard_map/psum | solution.py:198
  435.8 9.4 %reshape.681 = f32[48,25600]{1,0:T(8,128)} reshape(f32[8,6,160,160]{3,2,1,0:T(8,128)} %convolution_bitcast_fusion.1) | data formatting | bytes 9830400 | tf_op jit(solution)/shard_map/reshape | solution.py:23
  450.8 10.7 %gather_fusion.2 = f32[64,25600]{1,0:T(8,128)} fusion(f32[64,25600]{1,0:T(8,128)} %pad_maximum_fusion.1, s32[1024]{0:T(1024)S(1)} %pad_clamp_fusion.1), kind=kCustom, calls=%fused_computation.2 | custom fusion | bytes 13107456 | tf_op jit(solution)/shard_map/gather | solution.py:295
  467.0 11.1 %reshape.683 = f32[8,160,8,160]{3,2,1,0:T(8,128)} reshape(f32[1280,1280]{1,0:T(8,128)} %fusion.96) | data formatting | bytes 13107200 | tf_op jit(solution)/shard_map/reshape | solution.py:22
  478.1 11.2 %copy.122 = f32[8,8,160,160]{3,2,1,0:T(8,128)} copy(f32[8,8,160,160]{3,1,2,0:T(8,128)} %bitcast.359) | data formatting | bytes 13107200 | tf_op jit(solution)/shard_map/transpose | solution.py:23
  489.3 12.1 %reshape.684 = f32[64,25600]{1,0:T(8,128)} reshape(f32[8,8,160,160]{3,2,1,0:T(8,128)} %copy.122) | data formatting | bytes 13107200 | tf_op jit(solution)/shard_map/reshape | solution.py:23
  507.1 12.0 %reshape.685 = f32[64,25600]{1,0:T(8,128)} reshape(f32[8,8,160,160]{3,2,1,0:T(8,128)} %convolution_bitcast_fusion) | data formatting | bytes 13107200 | tf_op jit(solution)/shard_map/reshape | solution.py:23
  519.1 11.0 %pad_maximum_fusion = f32[128,25600]{1,0:T(8,128)} fusion(f32[64,25600]{1,0:T(8,128)} %reshape.685, f32[64,25600]{1,0:T(8,128)} %reshape.684), kind=kLoop, calls=%fused_computation.4 | loop fusion | flops 3276800 | bytes 26214400 | tf_op jit(solution)/shard_map/concatenate | solution.py:216
  530.1 19.3 %gather_fusion.3 = f32[128,25600]{1,0:T(8,128)} fusion(f32[128,25600]{1,0:T(8,128)} %pad_maximum_fusion, s32[1024]{0:T(1024)S(1)} %pad_clamp_fusion), kind=kCustom, calls=%fused_computation.3 | custom fusion | bytes 26214912 | tf_op jit(solution)/shard_map/gather | solution.py:216
  562.5 11.3 %psum.86 = bf16[2,27,80]{2,1,0:T(8,128)(2,1)S(1)} all-reduce(bf16[2,27,80]{2,1,0:T(8,128)(2,1)S(1)} %pad_maximum_fusion.2), channel_id=1, replica_groups=mesh['dp'=8,'mp'=4] {'mp'}, use_global_device_ids=true, to_apply=%region_32.33 | all-reduce | flops 4320 | bytes 17280 | tf_op jit(solution)/shard_map/psum | solution.py:287
  577.1 40.7 %all-reduce = (f32[2,1280]{1,0:T(2,128)}, f32[2,1280]{1,0:T(2,128)}, f32[2,1280]{1,0:T(2,128)}, f32[960]{0:T(1024)}, f32[1280]{0:T(1024)}, /*index=5*/f32[2,27,80]{2,1,0:T(8,128)S(1)}) all-reduce(f32[2,1280]{1,0:T(2,128)S(1)} %pad_maximum_fusion.3, f32[2,1280]{1,0:T(2,128)S(1)} %pad_maximum_fusion.4, ...), channel_id=1, replica_groups=mesh['dp'=8,'mp'=4] {'dp'}, use_global_device_ids=true, to_apply=%region_21.22 | all-reduce | flops 14240 | bytes 105280 | tf_op jit(solution)/shard_map/psum | solution.py:303
  647.8 154.6 %reduce-scatter.5.cloned.1.call-done = f32[1,16,25600]{2,1,0:T(8,128)} async-done(((f32[1,128,25600]{2,1,0:T(8,128)}), f32[1,16,25600]{2,1,0:T(8,128)}) %reduce-scatter.5.cloned.1.call-update) | async-done | bytes 1638416 | tf_op jit(solution)/shard_map/reduce_scatter | solution.py:300
  806.3 8.1 fusion.111
  (278 shorter events, 285.4 us)
Async XLA Ops:
  8.0 160.3 %all-reduce.6.cloned.1.call-start = ((), (), s32[]{:S(2)}) async-start(), calls=%async_computation.2 | async-start | bytes 1024000 | tf_op jit(solution)/shard_map/psum | solution.py:189
  10.0 20.8 %collective-permute-start = (bf16[1,8,25600]{2,1,0:T(8,128)(2,1)}, bf16[1,8,25600]{2,1,0:T(8,128)(2,1)}, u32[]{:S(2)}, u32[]{:S(2)}) collective-permute-start(bf16[1,8,25600]{2,1,0:T(8,128)(2,1)} %get-tuple-element.116), channel_id=1, source_target_pairs={{0,4},{4,8},{8,12},{12,16},{16,20},{20,24},{24,28},{28,0},{1,5},{5... | collective-permute-start | bytes 1228808 | tf_op jit(solution)/shard_map/ppermute | solution.py:114
  13.0 20.3 %collective-permute-start.1 = (bf16[1,8,25600]{2,1,0:T(8,128)(2,1)}, bf16[1,8,25600]{2,1,0:T(8,128)(2,1)}, u32[]{:S(2)}, u32[]{:S(2)}) collective-permute-start(bf16[1,8,25600]{2,1,0:T(8,128)(2,1)} %get-tuple-element.116), channel_id=1, source_target_pairs={{0,28},{4,0},{8,4},{12,8},{16,12},{20,16},{24,20},{28,24},{1,29},{... | collective-permute-start | bytes 1228808 | tf_op jit(solution)/shard_map/ppermute | solution.py:119
  16.1 55.0 %copy-start.33 = (s32[14,14]{1,0:T(8,128)}, s32[14,14]{1,0:T(8,128)S(1)}, u32[]{:S(2)}) copy-start(s32[14,14]{1,0:T(8,128)S(1)} %subtract_add_fusion) | copy-start | bytes 2356
  19.4 87.6 %copy-start.37 = (f32[196]{0:T(256)}, f32[196]{0:T(256)S(1)}, u32[]{:S(2)}) copy-start(f32[196]{0:T(256)S(1)} %broadcast_multiply_fusion.5) | copy-start | bytes 2356
  21.3 337.8 %copy-start.39 = (f32[1,196]{1,0:T(1,128)}, f32[1,196]{1,0:T(1,128)S(1)}, u32[]{:S(2)}) copy-start(f32[1,196]{1,0:T(1,128)S(1)} %convert_element_type.176) | copy-start | bytes 2356
  22.7 84.3 %copy-start.44 = (f32[196]{0:T(256)}, f32[196]{0:T(256)S(1)}, u32[]{:S(2)}) copy-start(f32[196]{0:T(256)S(1)} %add_rsqrt_fusion.1) | copy-start | bytes 2356
  30.8 19.4 %collective-permute-start.2 = (bf16[1,8,25600]{2,1,0:T(8,128)(2,1)}, bf16[1,8,25600]{2,1,0:T(8,128)(2,1)S(1)}, u32[]{:S(2)}, u32[]{:S(2)}) collective-permute-start(bf16[1,8,25600]{2,1,0:T(8,128)(2,1)} %collective-permute-done), channel_id=1, source_target_pairs={{0,4},{4,8},{8,12},{12,16},{16,20},{20,24},{24,28},{28,0},{1,5},{5... | collective-permute-start | bytes 1228808 | tf_op jit(solution)/shard_map/ppermute | solution.py:114
  33.3 19.3 %collective-permute-start.3 = (bf16[1,8,25600]{2,1,0:T(8,128)(2,1)}, bf16[1,8,25600]{2,1,0:T(8,128)(2,1)S(1)}, u32[]{:S(2)}, u32[]{:S(2)}) collective-permute-start(bf16[1,8,25600]{2,1,0:T(8,128)(2,1)} %collective-permute-done.1), channel_id=1, source_target_pairs={{0,28},{4,0},{8,4},{12,8},{16,12},{20,16},{24,20},{28,24},{1,29},{... | collective-permute-start | bytes 1228808 | tf_op jit(solution)/shard_map/ppermute | solution.py:119
  50.3 18.3 %collective-permute-start.4 = (bf16[1,8,25600]{2,1,0:T(8,128)(2,1)S(1)}, bf16[1,8,25600]{2,1,0:T(8,128)(2,1)S(1)}, u32[]{:S(2)}, u32[]{:S(2)}) collective-permute-start(bf16[1,8,25600]{2,1,0:T(8,128)(2,1)S(1)} %collective-permute-done.2), channel_id=1, source_target_pairs={{0,4},{4,8},{8,12},{12,16},{16,20},{20,24},{24,28},{28,0},{1,5},{5... | collective-permute-start | bytes 1228808 | tf_op jit(solution)/shard_map/ppermute | solution.py:114
  52.7 18.5 %collective-permute-start.5 = (bf16[1,8,25600]{2,1,0:T(8,128)(2,1)S(1)}, bf16[1,8,25600]{2,1,0:T(8,128)(2,1)S(1)}, u32[]{:S(2)}, u32[]{:S(2)}) collective-permute-start(bf16[1,8,25600]{2,1,0:T(8,128)(2,1)S(1)} %collective-permute-done.3), channel_id=1, source_target_pairs={{0,28},{4,0},{8,4},{12,8},{16,12},{20,16},{24,20},{28,24},{1,29},{... | collective-permute-start | bytes 1228808 | tf_op jit(solution)/shard_map/ppermute | solution.py:119
  68.6 12.6 %collective-permute-start.6 = (bf16[1,8,25600]{2,1,0:T(8,128)(2,1)S(1)}, bf16[1,8,25600]{2,1,0:T(8,128)(2,1)S(1)}, u32[]{:S(2)}, u32[]{:S(2)}) collective-permute-start(bf16[1,8,25600]{2,1,0:T(8,128)(2,1)S(1)} %collective-permute-done.4), channel_id=1, source_target_pairs={{0,4},{4,8},{8,12},{12,16},{16,20},{20,24},{24,28},{28,0},{1,5},{5... | collective-permute-start | bytes 1228808 | tf_op jit(solution)/shard_map/ppermute | solution.py:114
  110.1 254.7 %copy-start.15 = (bf16[196,960]{0,1:T(8,128)(2,1)}, bf16[196,960]{0,1:T(8,128)(2,1)S(1)}, u32[]{:S(2)}) copy-start(bf16[196,960]{0,1:T(8,128)(2,1)S(1)} %copy.93) | copy-start | bytes 1128964
  136.3 103.5 %all-gather.2.cloned.1.call-start = ((), (), s32[]{:S(2)}) async-start(), calls=%async_computation.3 | async-start | bytes 7372800 | tf_op jit(solution)/shard_map/all_gather | solution.py:140
  138.8 218.6 %all-reduce.8.cloned.1.call-start = ((), (), s32[]{:S(2)}) async-start(), calls=%async_computation.4 | async-start | bytes 1024000 | tf_op jit(solution)/shard_map/psum | solution.py:219
  325.8 99.6 %all-reduce.10.cloned.1.call-start = ((), (), s32[]{:S(2)}) async-start(), calls=%async_computation.7 | async-start | bytes 2048000 | tf_op jit(solution)/shard_map/psum | solution.py:198
  388.9 229.5 %reduce-scatter.3.cloned.1.call-start = ((), (), s32[]{:S(2)}) async-start(), calls=%async_computation.5 | async-start | bytes 7372800 | tf_op jit(solution)/shard_map/reduce_scatter | solution.py:299
  393.9 31.5 %copy-start.24 = (bf16[1,196,1280]{2,1,0:T(8,128)(2,1)S(1)}, bf16[1,196,1280]{2,1,0:T(8,128)(2,1)}, u32[]{:S(2)}) copy-start(bf16[1,196,1280]{2,1,0:T(8,128)(2,1)} %param.23) | copy-start | bytes 1505284
  393.9 31.5 %copy-start.38 = (f32[196]{0:T(256)S(1)}, f32[196]{0:T(256)}, u32[]{:S(2)}) copy-start(f32[196]{0:T(256)} %copy-done.37) | copy-start | bytes 2356
  393.9 31.5 %copy-start.40 = (f32[1,196]{1,0:T(1,128)S(1)}, f32[1,196]{1,0:T(1,128)}, u32[]{:S(2)}) copy-start(f32[1,196]{1,0:T(1,128)} %copy-done.39) | copy-start | bytes 2356
  393.9 31.5 %copy-start.45 = (f32[196]{0:T(256)S(1)}, f32[196]{0:T(256)}, u32[]{:S(2)}) copy-start(f32[196]{0:T(256)} %copy-done.44) | copy-start | bytes 2356
  393.9 34.0 %copy-start.7 = (f32[196,1280]{1,0:T(8,128)S(1)}, f32[196,1280]{1,0:T(8,128)}, u32[]{:S(2)}) copy-start(f32[196,1280]{1,0:T(8,128)} %copy-done.6) | copy-start | bytes 3010564
  461.6 340.8 %reduce-scatter.5.cloned.1.call-start = ((), (), s32[]{:S(2)}) async-start(), calls=%async_computation.6 | async-start | bytes 14745600 | tf_op jit(solution)/shard_map/reduce_scatter | solution.py:300
  559.5 17.6 %copy-start.46 = (f32[1280]{0:T(1024)S(1)}, f32[1280]{0:T(1024)}, u32[]{:S(2)}) copy-start(f32[1280]{0:T(1024)} %get-tuple-element.130) | copy-start | bytes 15364
  (45 other events, 228.8 us)
Sparse Core Ops, SparseCore 0:
  136.4 31.8 all-reduce.5
  325.9 31.4 all-reduce.7
  389.1 36.3 all-reduce.9
Sparse Core Ops, SparseCore 1:
  139.6 100.2 all-gather.1
  461.7 122.5 reduce-scatter.2
  588.3 214.0 reduce-scatter.4
